TPU v7x, 512 devices: a whole 4x8x8 slice. The times are simulated.
512 devices in a mesh: gx: 8 (over x, core), gy: 64 (over y, z).
Axes of the slice: x: 4, y: 8, z: 8, core: 2. Of those that a mesh axis runs over, the one named last changes fastest.
Arguments:
- cell: int32 [16777216], P(('gx', 'gy')), may hold values from 0 to 524287
- vehicle: int32 [16777216], P(('gx', 'gy')), may hold values from 0 to 1023
- speed: float32 [16777216], P(('gx', 'gy')), may hold values from 0 to 64, as said below
Outputs:
- top_speed: float32 [524288], P(('gx', 'gy'))
- top_vehicle: int32 [524288], P(('gx', 'gy'))
Inputs may be any that keep to these rules, and one draw needn't show every extreme that they name: Every speed is a whole multiple of 1/1024.
All inputs are finite; a program needn't handle non-finite values.
Results may differ from a plain program's by a relative error of at most 0.0003.
Values sent between devices are 32-bit elements; how exact they have to be, the bound alone decides.
A program may use at most 64 MiB of HBM per device.

v0:
```python
import jax
import jax.numpy as jnp
from jax import lax
from jax.sharding import PartitionSpec as P

CELLS = 524288
VEHICLES = 1024


def swapped(block, axis, apart):
    count = lax.axis_size(axis)
    route = []
    for low in range(count):
        high = low | 1 << apart
        if high != low and high < count:
            route += [(low, high), (high, low)]
    return lax.ppermute(block, axis, route)


def combine(first, second):
    speed_a = first[0]
    speed_b = second[0]
    best = jnp.maximum(speed_a, speed_b)
    ident = jnp.where(
        speed_a > speed_b,
        first[1],
        jnp.where(speed_b > speed_a, second[1], jnp.minimum(first[1], second[1])),
    )
    return jnp.stack([best, ident])


def per_device(cell, vehicle, speed):
    local_best = jnp.full((CELLS,), -1.0, jnp.float32).at[cell].max(speed)
    chosen = jnp.where(speed == local_best[cell], vehicle, VEHICLES)
    local_ident = jnp.full((CELLS,), VEHICLES, jnp.int32).at[cell].min(chosen)
    paired = jnp.stack([local_best, local_ident.astype(jnp.float32)])
    outer = lax.axis_size("gx")
    inner = lax.axis_size("gy")
    nbits = (outer * inner).bit_length() - 1
    myself = lax.axis_index(("gx", "gy"))
    buffer = paired
    for level in reversed(range(nbits)):
        half = buffer.shape[1] // 2
        side = myself >> level & 1
        keep = lax.dynamic_slice_in_dim(buffer, side * half, half, 1)
        give = lax.dynamic_slice_in_dim(buffer, (1 - side) * half, half, 1)
        partner = swapped(give, ("gx", "gy"), level)
        buffer = combine(keep, partner)
    best = buffer[0]
    ident = buffer[1]
    lowest = ident.astype(jnp.int32)
    top_vehicle = jnp.where(lowest < VEHICLES, lowest, -1)
    return (best, top_vehicle)


def solution(mesh):
    placed = (P(("gx", "gy")), P(("gx", "gy")), P(("gx", "gy")))
    return jax.shard_map(
        per_device,
        mesh=mesh,
        in_specs=placed,
        out_specs=(P(("gx", "gy")), P(("gx", "gy"))),
        check_vma=False,
    )
```

profile of v0, /device:TPU:1, one launch (start us, length us, event | category | flops | bytes accessed | tf_op | source)
XLA Modules:
  0.0 693.6 jit_solution(7661752814337770442)
XLA Ops:
  0.6 0.9 broadcast_clamp_fusion
  1.6 171.8 %scatter_custom_fusion = f32[524288]{0:T(1024)S(1)} fusion(s32[32768]{0:T(1024)S(1)} %get-tuple-element.29, f32[32768]{0:T(1024)} %param.5, f32[]{:T(128)} %constant.25.clone.1), kind=kCustom, calls=%fused_computation.25 | custom fusion | flops 32768 | bytes 2097664 | tf_op jit(solution)/shard_map/scatter-max | solution.py:33
  173.4 0.0 copy-start
  173.4 0.0 copy-start.1
  173.5 180.5 %gather_fusion = f32[32768]{0:T(1024)S(1)} fusion(f32[524288]{0:T(1024)S(1)} %scatter_custom_fusion, s32[32768]{0:T(1024)S(1)} %get-tuple-element.28), kind=kCustom, calls=%fused_computation | custom fusion | bytes 393216 | tf_op jit(solution)/shard_map/gather | solution.py:34
  354.0 0.0 copy-done
  354.0 0.0 copy-done.1
  354.1 176.4 %scatter_custom_fusion.1 = s32[524288]{0:T(1024)} fusion(s32[32768]{0:T(1024)S(1)} %get-tuple-element.29, s32[32768]{0:T(1024)S(1)} %compare_select_fusion.13, s32[]{:T(128)} %constant.28.clone.1), kind=kCustom, calls=%fused_computation.23 | custom fusion | flops 32768 | bytes 2097156 | tf_op jit(solution)/shard_map/scatter-min | solution.py:35
  530.4 3.1 convert_element_type.6
  533.5 7.0 %fusion.1 = (f32[2,262144]{1,0:T(2,128)}, f32[2,262144]{1,0:T(2,128)}) fusion(s32[]{:T(128)S(6)} %select_n.148, f32[1,524288]{1,0:T(1,128)S(1)} %bitcast.5, f32[1,524288]{1,0:T(1,128)} %bitcast.6, s32[]{:T(128)S(6)} %select_n.149), kind=kLoop, calls=%fused_computation.14 | loop fusion | flops 1048576 | bytes 8388616 | tf_op jit(solution)/shard_map/stack | solution.py:36
  540.5 5.5 collective-permute-start
  546.0 42.3 %collective-permute-done = f32[2,262144]{1,0:T(2,128)S(1)} collective-permute-done((f32[2,262144]{1,0:T(2,128)}, f32[2,262144]{1,0:T(2,128)S(1)}, u32[]{:S(2)}, u32[]{:S(2)}) %collective-permute-start) | collective-permute-done | bytes 2097184 | tf_op jit(solution)/shard_map/ppermute | solution.py:17
  588.2 4.8 compare_select_fusion.1
  593.0 2.2 fusion.3
  595.3 6.5 collective-permute-start.1
  601.8 21.5 %collective-permute-done.1 = f32[2,131072]{1,0:T(2,128)S(1)} collective-permute-done((f32[2,131072]{1,0:T(2,128)S(1)}, f32[2,131072]{1,0:T(2,128)S(1)}, u32[]{:S(2)}, u32[]{:S(2)}) %collective-permute-start.1) | collective-permute-done | bytes 1048608 | tf_op jit(solution)/shard_map/ppermute | solution.py:17
  623.3 1.4 compare_select_fusion.3
  624.7 1.2 fusion.9
  625.8 4.3 collective-permute-start.2
  630.2 1.5 collective-permute-done.2
  631.7 0.7 compare_select_fusion.5
  632.4 0.6 fusion.11
  633.0 7.7 %collective-permute-start.3 = (f32[2,32768]{1,0:T(2,128)S(1)}, f32[2,32768]{1,0:T(2,128)S(1)}, u32[]{:S(2)}, u32[]{:S(2)}) collective-permute-start(f32[2,32768]{1,0:T(2,128)S(1)} %get-tuple-element.19), channel_id=1, source_target_pairs={{0,32},{32,0},{1,33},{33,1},{2,34},{34,2},{3,35},{35,3},{4,36},{36... | collective-permute-start | bytes 786440 | tf_op jit(solution)/shard_map/ppermute | solution.py:17
  640.7 8.0 %collective-permute-done.3 = f32[2,32768]{1,0:T(2,128)S(1)} collective-permute-done((f32[2,32768]{1,0:T(2,128)S(1)}, f32[2,32768]{1,0:T(2,128)S(1)}, u32[]{:S(2)}, u32[]{:S(2)}) %collective-permute-start.3) | collective-permute-done | bytes 262176 | tf_op jit(solution)/shard_map/ppermute | solution.py:17
  648.7 0.3 compare_select_fusion.7
  649.0 0.3 fusion.13
  649.4 8.4 %collective-permute-start.4 = (f32[2,16384]{1,0:T(2,128)S(1)}, f32[2,16384]{1,0:T(2,128)S(1)}, u32[]{:S(2)}, u32[]{:S(2)}) collective-permute-start(f32[2,16384]{1,0:T(2,128)S(1)} %get-tuple-element.23), channel_id=1, source_target_pairs={{0,16},{16,0},{1,17},{17,1},{2,18},{18,2},{3,19},{19,3},{4,20},{20... | collective-permute-start | bytes 393224 | tf_op jit(solution)/shard_map/ppermute | solution.py:17
  657.8 6.7 collective-permute-done.4
  664.5 0.2 compare_select_fusion.10
  664.7 0.2 fusion.15
  664.9 1.9 collective-permute-start.5
  666.8 3.1 collective-permute-done.5
  669.9 0.1 compare_select_fusion.12
  670.0 0.1 fusion.17
  670.1 10.6 %collective-permute-start.6 = (f32[2,4096]{1,0:T(2,128)S(1)}, f32[2,4096]{1,0:T(2,128)S(1)}, u32[]{:S(2)}, u32[]{:S(2)}) collective-permute-start(f32[2,4096]{1,0:T(2,128)S(1)} %get-tuple-element.33), channel_id=1, source_target_pairs={{0,4},{4,0},{1,5},{5,1},{2,6},{6,2},{3,7},{7,3},{8,12},{12,8},{9,1... | collective-permute-start | bytes 98312 | tf_op jit(solution)/shard_map/ppermute | solution.py:17
  680.8 1.3 collective-permute-done.6
  682.2 0.1 fusion.19
  682.3 4.4 collective-permute-start.7
  686.7 1.1 collective-permute-done.7
  687.8 0.1 fusion.21
  687.9 2.9 collective-permute-start.8
  690.9 1.5 collective-permute-done.8
  692.4 0.6 fusion.24
  693.0 0.6 compare_select_fusion.18
  (4 shorter events, 0.1 us)
Async XLA Ops:
  173.4 180.6 %copy-start = (f32[32768]{0:T(1024)S(1)}, f32[32768]{0:T(1024)}, u32[]{:S(2)}) copy-start(f32[32768]{0:T(1024)} %param.5) | copy-start | bytes 393220
  173.4 180.6 %copy-start.1 = (s32[32768]{0:T(1024)S(1)}, s32[32768]{0:T(1024)}, u32[]{:S(2)}) copy-start(s32[32768]{0:T(1024)} %param.4) | copy-start | bytes 393220
  540.5 47.7 %collective-permute-start = (f32[2,262144]{1,0:T(2,128)}, f32[2,262144]{1,0:T(2,128)S(1)}, u32[]{:S(2)}, u32[]{:S(2)}) collective-permute-start(f32[2,262144]{1,0:T(2,128)} %get-tuple-element.7), channel_id=1, source_target_pairs={{0,256},{256,0},{1,257},{257,1},{2,258},{258,2},{3,259},{259,3},{4... | collective-permute-start | bytes 6291464 | tf_op jit(solution)/shard_map/ppermute | solution.py:17
  595.3 28.0 %collective-permute-start.1 = (f32[2,131072]{1,0:T(2,128)S(1)}, f32[2,131072]{1,0:T(2,128)S(1)}, u32[]{:S(2)}, u32[]{:S(2)}) collective-permute-start(f32[2,131072]{1,0:T(2,128)S(1)} %get-tuple-element.11), channel_id=1, source_target_pairs={{0,128},{128,0},{1,129},{129,1},{2,130},{130,2},{3,131},{131,3},{4... | collective-permute-start | bytes 3145736 | tf_op jit(solution)/shard_map/ppermute | solution.py:17
  625.8 5.8 collective-permute-start.2
  633.0 15.7 %collective-permute-start.3 = (f32[2,32768]{1,0:T(2,128)S(1)}, f32[2,32768]{1,0:T(2,128)S(1)}, u32[]{:S(2)}, u32[]{:S(2)}) collective-permute-start(f32[2,32768]{1,0:T(2,128)S(1)} %get-tuple-element.19), channel_id=1, source_target_pairs={{0,32},{32,0},{1,33},{33,1},{2,34},{34,2},{3,35},{35,3},{4,36},{36... | collective-permute-start | bytes 786440 | tf_op jit(solution)/shard_map/ppermute | solution.py:17
  649.4 15.1 %collective-permute-start.4 = (f32[2,16384]{1,0:T(2,128)S(1)}, f32[2,16384]{1,0:T(2,128)S(1)}, u32[]{:S(2)}, u32[]{:S(2)}) collective-permute-start(f32[2,16384]{1,0:T(2,128)S(1)} %get-tuple-element.23), channel_id=1, source_target_pairs={{0,16},{16,0},{1,17},{17,1},{2,18},{18,2},{3,19},{19,3},{4,20},{20... | collective-permute-start | bytes 393224 | tf_op jit(solution)/shard_map/ppermute | solution.py:17
  664.9 5.0 collective-permute-start.5
  670.1 12.0 %collective-permute-start.6 = (f32[2,4096]{1,0:T(2,128)S(1)}, f32[2,4096]{1,0:T(2,128)S(1)}, u32[]{:S(2)}, u32[]{:S(2)}) collective-permute-start(f32[2,4096]{1,0:T(2,128)S(1)} %get-tuple-element.33), channel_id=1, source_target_pairs={{0,4},{4,0},{1,5},{5,1},{2,6},{6,2},{3,7},{7,3},{8,12},{12,8},{9,1... | collective-permute-start | bytes 98312 | tf_op jit(solution)/shard_map/ppermute | solution.py:17
  682.3 5.5 collective-permute-start.7
  687.9 4.4 collective-permute-start.8
where the time goes:
time: 697 us; the launch traced here: 694 us
  other arithmetic  373 us (54%)
  local copies, waits for them, and re-layouts  181 us (26%)
  waiting for transfers between devices  86.9 us (12%)
  starting transfers between devices  52.3 us (8%)
    gather x1, local copies, waits for them, and re-layouts, per_device(): chosen = jnp.where(speed == local_best[cell], vehicle, VEHICLES)  181 us
    another operation x1, other arithmetic, per_device(): local_ident = jnp.full((CELLS,), VEHICLES, jnp.int32).at[cell].min(chosen)  176 us
    another operation x1, other arithmetic, per_device(): local_best = jnp.full((CELLS,), -1.0, jnp.float32).at[cell].max(speed)  172 us
    ppermute x9, waiting for transfers between devices, swapped(): return lax.ppermute(block, axis, route)  86.9 us
    ppermute x9, starting transfers between devices, swapped(): return lax.ppermute(block, axis, route)  52.3 us
  transfers between devices with their start and end apart: 9, of which 9 were waited for; matrix products, arithmetic and copies ran while one was open for 0% of the time, Pallas kernels for 0%

commit v1 on v0

--- a/solution.py
+++ b/solution.py
@@ -1,10 +1,17 @@
 import jax
 import jax.numpy as jnp
+import numpy as np
 from jax import lax
+from jax.experimental import pallas as pl
+from jax.experimental.pallas import tpu as pltpu
 from jax.sharding import PartitionSpec as P
 
 CELLS = 524288
 VEHICLES = 1024
+MESH = pl.DeviceIdType.MESH
+SIGN = np.int32(-(2**31))
+CAP = 2048
+EMPTY = 131072
 
 
 def swapped(block, axis, apart):
@@ -29,7 +36,7 @@
     return jnp.stack([best, ident])
 
 
-def per_device(cell, vehicle, speed):
+def dense_path(cell, vehicle, speed):
     local_best = jnp.full((CELLS,), -1.0, jnp.float32).at[cell].max(speed)
     chosen = jnp.where(speed == local_best[cell], vehicle, VEHICLES)
     local_ident = jnp.full((CELLS,), VEHICLES, jnp.int32).at[cell].min(chosen)
@@ -47,10 +54,528 @@
         partner = swapped(give, ("gx", "gy"), level)
         buffer = combine(keep, partner)
     best = buffer[0]
-    ident = buffer[1]
-    lowest = ident.astype(jnp.int32)
-    top_vehicle = jnp.where(lowest < VEHICLES, lowest, -1)
-    return (best, top_vehicle)
+    lowest = buffer[1].astype(jnp.int32)
+    return best, jnp.where(lowest < VEHICLES, lowest, -1)
+
+
+def lanes():
+    return lax.broadcasted_iota(jnp.int32, (8, 128), 1)
+
+
+def subs():
+    return lax.broadcasted_iota(jnp.int32, (8, 128), 0)
+
+
+def lane_xor(x, index):
+    return jnp.take_along_axis(x, index, axis=1)
+
+
+def sub_xor(x, bit):
+    d = 1 << bit
+    if d == 4:
+        return pltpu.roll(x, 4, 0)
+    return jnp.where((subs() & d) != 0, pltpu.roll(x, d, 0), pltpu.roll(x, 8 - d, 0))
+
+
+def above(c1, k1, c2, k2):
+    return (c1 > c2) | ((c1 == c2) & (k1 > k2))
+
+
+def order_pair(a, b, down):
+    swap = above(*a, *b)
+    if down is True:
+        a, b = b, a
+    elif down is not False:
+        swap = swap ^ down
+    low = tuple(jnp.where(swap, y, x) for x, y in zip(a, b))
+    high = tuple(jnp.where(swap, x, y) for x, y in zip(a, b))
+    return low, high
+
+
+def order_cross(x, y, wants_max):
+    swap = above(*x, *y) ^ wants_max
+    return tuple(jnp.where(swap, q, p) for p, q in zip(x, y))
+
+
+def move_pair(a, b, bit):
+    mask = SIGN | np.int32(1 << bit)
+    one = mask
+    ma, mb = a[0] & mask, b[0] & mask
+    a0, b0 = ma == SIGN, mb == SIGN
+    a1, b1 = ma == one, mb == one
+    low = (jnp.where(b0, b[0], jnp.where(a0, a[0], 0)), jnp.where(b0, b[1], a[1]))
+    high = (jnp.where(a1, a[0], jnp.where(b1, b[0], 0)), jnp.where(a1, a[1], b[1]))
+    return low, high
+
+
+def move_cross(x, y, bit, here):
+    mask = SIGN | np.int32(1 << bit)
+    mx, my = (x[0] & mask) == here, (y[0] & mask) == here
+    return jnp.where(my, y[0], jnp.where(mx, x[0], 0)), jnp.where(my, y[1], x[1])
+
+
+def get(refs, v):
+    return refs[0][v], refs[1][v]
+
+
+def put(refs, v, pair):
+    refs[0][v] = pair[0]
+    refs[1][v] = pair[1]
+
+
+def register_steps(refs, group_bits, count, bits, step):
+    for base in range(count):
+        if any(base >> b & 1 for b in group_bits):
+            continue
+        members = [base]
+        for b in group_bits:
+            members += [m | 1 << b for m in members]
+        held = {m: get(refs, m) for m in members}
+        for b in bits:
+            for m in members:
+                if not m >> b & 1:
+                    held[m], held[m | 1 << b] = step(held[m], held[m | 1 << b], b, m)
+        for m in members:
+            put(refs, m, held[m])
+
+
+def cross_steps(refs, count, steps):
+    for step in steps:
+        for v in range(count):
+            put(refs, v, step(get(refs, v), v))
+
+
+def batcher(n):
+    pairs = []
+
+    def merge(lo, n, r):
+        m = r * 2
+        if m < n:
+            merge(lo, n, m)
+            merge(lo + r, n, m)
+            for i in range(lo + r, lo + n - r, m):
+                pairs.append((i, i + r))
+        else:
+            pairs.append((lo, lo + r))
+
+    def sort(lo, n):
+        if n > 1:
+            m = n // 2
+            sort(lo, m)
+            sort(lo + m, m)
+            merge(lo, n, 1)
+
+    sort(0, n)
+    return pairs
+
+
+def total(x):
+    s = jnp.sum(x.astype(jnp.float32), axis=0, keepdims=True)
+    s = jnp.sum(s, axis=1, keepdims=True)
+    return jnp.broadcast_to(s, (8, 128)).astype(jnp.int32)
+
+
+def xor_prefix(x, order):
+    lane, sub = lanes(), subs()
+    before, block = jnp.zeros_like(x), x
+    for kind, i in order:
+        if kind == "s":
+            other, bit = sub_xor(block, i), (sub >> i) & 1
+        else:
+            other, bit = lane_xor(block, lane ^ (1 << i)), (lane >> i) & 1
+        before = before + jnp.where(bit == 1, other, 0)
+        block = block + other
+    return before, block
+
+
+def sort_events(cell, vehicle, speed, A, B):
+    lane, sub = lanes(), subs()
+    R = (A, B)
+    flip = -(sub & 1)
+    held = []
+    for v in range(32):
+        c = cell[v]
+        c = (
+            (c & 0x7E000 | ((c >> 10) & 1))
+            | ((c & 0x1800) | ((c & 7) << 8))
+            | (((c >> 2) & 0xE0) | ((c >> 2) & 0x1E))
+        )
+        k = (speed[v] * 1024.0).astype(jnp.int32) * 1024 + (1023 - vehicle[v])
+        held.append((c ^ flip, k ^ flip))
+    for i, j in batcher(32):
+        held[i], held[j] = order_pair(held[i], held[j], False)
+    for v in range(32):
+        put(R, v, (held[v][0] ^ flip, held[v][1] ^ flip))
+
+    def tail(down):
+        register_steps(R, (3, 4), 32, (4, 3), lambda a, b, *_: order_pair(a, b, down))
+        register_steps(R, (0, 1, 2), 32, (2, 1, 0), lambda a, b, *_: order_pair(a, b, down))
+
+    def sub_step(i, down):
+        wants = (((sub >> i) & 1) == 1) ^ down
+        return lambda x, v: order_cross(x, (sub_xor(x[0], i), sub_xor(x[1], i)), wants)
+
+    for top in (1, 2, 3):
+        down = ((sub >> top) & 1) == 1 if top < 3 else (lane & 1) == 1
+        cross_steps(R, 32, [sub_step(i, down) for i in reversed(range(top))])
+        tail(down)
+
+    def stage(s, _):
+        turned = (lane >> (s + 1)) & 1
+        down = turned == 1
+
+        def lane_step(n, _):
+            i = s - n
+            index = lane ^ (1 << i)
+            wants = (((lane >> i) & 1) ^ turned) == 1
+            cross_steps(
+                R, 32, [lambda x, v: order_cross(x, (lane_xor(x[0], index), lane_xor(x[1], index)), wants)]
+            )
+            return 0
+
+        lax.fori_loop(0, s + 1, lane_step, 0)
+        cross_steps(R, 32, [sub_step(i, down) for i in (2, 1, 0)])
+        tail(down)
+        return 0
+
+    lax.fori_loop(0, 7, stage, 0)
+
+
+def list_rank(v):
+    lane = lanes()
+    return (v >> 1) * CAP + ((lane & 7) << 8) + (subs() << 5) + ((lane >> 3) << 1) + (v & 1)
+
+
+LIST_BITS = [("v", 0), ("l", 3), ("l", 4), ("l", 5), ("l", 6), ("s", 0), ("s", 1), ("s", 2), ("l", 0), ("l", 1), ("l", 2),
+             ("v", 1), ("v", 2), ("v", 3)]
+
+
+def route(refs, count, order, shift=16):
+    lane, sub = lanes(), subs()
+    at = 0
+    while at < len(order):
+        bit, kind, i = order[at]
+        if kind == "v":
+            run = [order[at]]
+            while at + len(run) < len(order) and order[at + len(run)][1] == "v" and len(run) < 3:
+                run.append(order[at + len(run)])
+            number = {i: shift + b for b, _, i in run}
+            register_steps(
+                refs, tuple(i for _, _, i in run), count, tuple(i for _, _, i in run),
+                lambda a, b, i, _: move_pair(a, b, number[i]),
+            )
+            at += len(run)
+            continue
+        b = shift + bit
+        if kind == "s":
+            here = SIGN | (((sub >> i) & 1) << b)
+            step = lambda x, v: move_cross(x, (sub_xor(x[0], i), sub_xor(x[1], i)), b, here)
+        else:
+            here = SIGN | (((lane >> i) & 1) << b)
+            index = lane ^ (1 << i)
+            step = lambda x, v: move_cross(x, (lane_xor(x[0], index), lane_xor(x[1], index)), b, here)
+        cross_steps(refs, count, [step])
+        at += 1
+
+
+def group_starts(groups, valid, count):
+    starts = [jnp.zeros((8, 128), jnp.int32)]
+    for j in range(1, 9):
+        t = jnp.zeros((8, 128), jnp.int32)
+        for v in range(count):
+            t = t + jnp.where(valid[v] & (groups[v] < j), 1, 0)
+        starts.append(total(t))
+    return starts
+
+
+def crowded(starts):
+    most = jnp.zeros((8, 128), jnp.int32)
+    for j in range(8):
+        most = jnp.maximum(most, starts[j + 1] - starts[j])
+    return (most > CAP).astype(jnp.int32)
+
+
+def offsets(groups, starts):
+    moved = jnp.zeros((8, 128), jnp.int32)
+    for j in range(1, 8):
+        moved = jnp.where(groups == j, j * CAP - starts[j], moved)
+    return moved
+
+
+def compact_events(A, B, S, T):
+    lane, sub = lanes(), subs()
+    first = A[0]
+    down1 = pltpu.roll(first, 7, 0)
+    follow = jnp.where(sub == 7, pltpu.roll(down1, 127, 1), down1)
+    last = (sub == 7) & (lane == 127)
+    run = jnp.zeros((8, 128), jnp.int32)
+    keeps, ranks = [], []
+    cells = [A[v] for v in range(32)]
+    for v in range(32):
+        nxt = cells[v + 1] if v < 31 else follow
+        keep = cells[v] != nxt
+        if v == 31:
+            keep = keep | last
+        keeps.append(keep)
+        ranks.append(run)
+        run = run + keep.astype(jnp.int32)
+    before, every = xor_prefix(run, [("s", 0), ("s", 1), ("s", 2)] + [("l", i) for i in range(7)])
+    for v in range(32):
+        c = cells[v]
+        w1 = SIGN | ((before + ranks[v]) << 16) | (c & 0xFFFF)
+        A[v] = jnp.where(keeps[v], w1, 0)
+        B[v] = B[v] | ((c >> 16) << 27)
+    order = [(i, "v", i) for i in range(5)] + [(5 + i, "s", i) for i in range(3)] + [(8 + i, "l", i) for i in range(7)]
+    route((A, B), 32, order)
+    low = lane < 64
+    for v in range(16):
+        for X, Y in ((A, S), (B, T)):
+            Y[v] = jnp.where(low, X[v], pltpu.roll(X[v + 16], 64, 1))
+    for j in range(3):
+        d = 8 << j
+        bit = (lane & d) != 0
+        for v in range(16):
+            w = v | 2 << j
+            if w == v:
+                continue
+            for Y in (S, T):
+                a, b = Y[v], Y[w]
+                Y[v] = jnp.where(bit, pltpu.roll(b, d, 1), a)
+                Y[w] = jnp.where(bit, b, pltpu.roll(a, 128 - d, 1))
+    valid = [S[v] < 0 for v in range(16)]
+    groups = [T[v] >> 27 for v in range(16)]
+    starts = group_starts(groups, valid, 16)
+    flag = crowded(starts) | (every > 8 * CAP).astype(jnp.int32)
+    for v in range(16):
+        target = list_rank(v) + offsets(groups[v], starts)
+        S[v] = jnp.where(valid[v], SIGN | (target << 16) | (S[v] & 0xFFFF), 0)
+        T[v] = T[v] & 0x7FFFFFF
+    return flag
+
+
+def expand_lists(S, T):
+    route((S, T), 16, [(b, *LIST_BITS[b]) for b in reversed(range(14))])
+
+
+def pack_messages(S, T, out):
+    for v in range(16):
+        g, h = v >> 1, v & 1
+        w, k = S[v], T[v]
+        out[g, h] = jnp.where(w < 0, w & 0xFFFF, EMPTY).astype(jnp.float32)
+        out[g, 2 + h] = (k >> 10).astype(jnp.float32) * (1.0 / 1024.0)
+        out[g, 4 + h] = (1023 - (k & 1023)).astype(jnp.float32)
+
+
+def key_of(speed, vehicle):
+    return (speed * 1024.0).astype(jnp.int32) * 1024 + (1023 - vehicle.astype(jnp.int32))
+
+
+def merge_lists(inbox, S, T):
+    lane, sub = lanes(), subs()
+    back = 127 - lane
+    R = (S, T)
+    for s in range(8):
+        for h in range(2):
+            pair = (inbox[s, h].astype(jnp.int32), key_of(inbox[s, 2 + h], inbox[s, 4 + h]))
+            if s & 1:
+                pair = tuple(lane_xor(sub_xor(sub_xor(sub_xor(x, 0), 1), 2), back) for x in pair)
+                put(R, 2 * s + 1 - h, pair)
+            else:
+                put(R, 2 * s + h, pair)
+    for level in (1, 2, 3):
+        down = (lambda v: bool(v >> (level + 1) & 1)) if level < 3 else (lambda v: False)
+        bits = tuple(reversed(range(1, level + 1)))
+        register_steps(R, bits, 16, bits, lambda a, b, i, m: order_pair(a, b, down(m)))
+        for kind, i in reversed(LIST_BITS[1:11]):
+            if kind == "s":
+                wants = {False: ((sub >> i) & 1) == 1, True: ((sub >> i) & 1) == 0}
+                step = lambda x, v: order_cross(x, (sub_xor(x[0], i), sub_xor(x[1], i)), wants[down(v)])
+            else:
+                wants = {False: ((lane >> i) & 1) == 1, True: ((lane >> i) & 1) == 0}
+                index = lane ^ (1 << i)
+                step = lambda x, v: order_cross(x, (lane_xor(x[0], index), lane_xor(x[1], index)), wants[down(v)])
+            cross_steps(R, 16, [step])
+        register_steps(R, (0,), 16, (0,), lambda a, b, i, m: order_pair(a, b, down(m)))
+
+
+def regroup(S, T):
+    cells = [S[v] for v in range(16)]
+    valid = [c < EMPTY for c in cells]
+    groups = [c >> 13 for c in cells]
+    starts = group_starts(groups, valid, 16)
+    for v in range(16):
+        target = list_rank(v) + offsets(groups[v], starts)
+        S[v] = jnp.where(valid[v], SIGN | (target << 16) | (cells[v] & 0x1FFF), 0)
+    flag = crowded(starts)
+    expand_lists(S, T)
+    return flag
+
+
+def to_table(S, T):
+    lane, sub = lanes(), subs()
+    cells = [S[v] for v in range(16)]
+    keeps = []
+    for p in range(8):
+        even, odd = cells[2 * p], cells[2 * p + 1]
+        keeps.append((even != odd) & (even < EMPTY))
+        ahead = pltpu.roll(even, 120, 1)
+        wrapped = pltpu.roll(ahead, 7, 0)
+        carried = pltpu.roll(wrapped, 127, 1)
+        if p < 7:
+            entry = jnp.broadcast_to(cells[2 * p + 2][0:1, 0:1], (8, 128))
+            carried = jnp.where((lane & 7) == 7, entry, carried)
+        nxt = jnp.where(lane >= 120, jnp.where(sub == 7, carried, wrapped), ahead)
+        keep = odd != nxt
+        if p == 7:
+            keep = keep | ((lane == 127) & (sub == 7))
+        keeps.append(keep & (odd < EMPTY))
+    done = jnp.zeros((8, 128), jnp.int32)
+    order = [("l", 3), ("l", 4), ("l", 5), ("l", 6), ("s", 0), ("s", 1), ("s", 2), ("l", 0), ("l", 1), ("l", 2)]
+    for p in range(8):
+        even, odd = (keeps[2 * p + h].astype(jnp.int32) for h in range(2))
+        before, block = xor_prefix(even + odd, order)
+        before = before + done
+        done = done + block
+        S[2 * p] = jnp.where(keeps[2 * p], SIGN | (before << 16) | cells[2 * p], 0)
+        S[2 * p + 1] = jnp.where(keeps[2 * p + 1], SIGN | ((before + even) << 16) | cells[2 * p + 1], 0)
+    route((S, T), 16, [(b, *LIST_BITS[b]) for b in range(14)])
+    for v in range(8):
+        w = S[v]
+        S[v] = jnp.where(w < 0, SIGN | ((w & 0x1FFF) << 16), 0)
+    route((S, T), 8, [(b, *LIST_BITS[b]) for b in reversed(range(13))])
+
+
+def exchange_kernel(cell, vehicle, speed, best, ident, flags, A, B, S, T, out1, in1, out2, in2, out3, in3, mark, marks1,
+                    mark2, marks2, send, recv):
+    gx, gy = lax.axis_index("gx"), lax.axis_index("gy")
+    y, z = gy // 8, gy % 8
+
+    def peer(phase, j):
+        if phase == 0:
+            return (gx ^ j, gy)
+        if phase == 1:
+            return (gx, (y ^ j) * 8 + z)
+        return (gx, y * 8 + (z ^ j))
+
+    barrier = pltpu.get_barrier_semaphore()
+    for phase in range(3):
+        for j in range(1, 8):
+            pl.semaphore_signal(barrier, inc=1, device_id=peer(phase, j), device_id_type=MESH)
+
+    def copies(lane_of, phase, source, target):
+        made = []
+        for j in range(1, 8):
+            made.append(
+                pltpu.make_async_remote_copy(
+                    src_ref=source(j),
+                    dst_ref=target.at[j],
+                    send_sem=send.at[lane_of, j],
+                    recv_sem=recv.at[lane_of, j],
+                    device_id=peer(phase, j),
+                    device_id_type=MESH,
+                )
+            )
+        return made
+
+    sort_events(cell, vehicle, speed, A, B)
+    flag = compact_events(A, B, S, T)
+    expand_lists(S, T)
+    pack_messages(S, T, out1)
+    pl.semaphore_wait(barrier, 21)
+    first = copies(0, 0, lambda j: out1.at[gx ^ j], in1)
+    for c in first:
+        c.start()
+    in1[0] = out1[gx]
+    for c in first:
+        c.wait_recv()
+
+    merge_lists(in1, S, T)
+    flag = flag | regroup(S, T)
+    mark[...] = flag.astype(jnp.float32)
+    pack_messages(S, T, out2)
+    second = copies(1, 1, lambda j: out2.at[y ^ j], in2)
+    for c in second:
+        c.start()
+    flags1 = copies(2, 0, lambda j: mark, marks1)
+    for c in flags1:
+        c.start()
+    in2[0] = out2[y]
+    for c in flags1:
+        c.wait_recv()
+    seen = mark[...]
+    for j in range(1, 8):
+        seen = jnp.maximum(seen, marks1[j])
+    mark2[...] = seen
+    flags2 = copies(3, 1, lambda j: mark2, marks2)
+    for c in flags2:
+        c.start()
+    for c in second:
+        c.wait_recv()
+
+    merge_lists(in2, S, T)
+    to_table(S, T)
+    for c in flags2:
+        c.wait_recv()
+    for j in range(1, 8):
+        seen = jnp.maximum(seen, marks2[j])
+    for v in range(8):
+        there, k = S[v] < 0, T[v]
+        out3[v, 0] = jnp.where(there, (k >> 10).astype(jnp.float32) * (1.0 / 1024.0), -1.0)
+        out3[v, 1] = jnp.where(there, (1023 - (k & 1023)).astype(jnp.float32), 1024.0)
+        out3[v, 2] = seen
+    third = copies(4, 2, lambda j: out3.at[z ^ j], in3)
+    for c in third:
+        c.start()
+    in3[0] = out3[z]
+    for c in third:
+        c.wait_recv()
+    k = key_of(in3[0, 0], in3[0, 1])
+    for j in range(1, 8):
+        k = jnp.maximum(k, key_of(in3[j, 0], in3[j, 1]))
+        seen = jnp.maximum(seen, in3[j, 2])
+    best[...] = jnp.where(k < 0, -1.0, (k >> 10).astype(jnp.float32) * (1.0 / 1024.0))
+    ident[...] = jnp.where(k < 0, -1, 1023 - (k & 1023))
+    flags[...] = seen
+    for group in (first, second, flags1, flags2, third):
+        for c in group:
+            c.wait_send()
+
+
+def words(*shape):
+    return pltpu.VMEM(shape + (8, 128), jnp.float32)
+
+
+def sparse_path(cell, vehicle, speed):
+    whole = pl.BlockSpec(memory_space=pltpu.VMEM)
+    ints = lambda n: pltpu.VMEM((n, 8, 128), jnp.int32)
+    return pl.pallas_call(
+        exchange_kernel,
+        out_shape=(
+            jax.ShapeDtypeStruct((8, 128), jnp.float32),
+            jax.ShapeDtypeStruct((8, 128), jnp.int32),
+            jax.ShapeDtypeStruct((8, 128), jnp.float32),
+        ),
+        in_specs=[whole] * 3,
+        out_specs=(whole,) * 3,
+        scratch_shapes=[
+            ints(32), ints(32), ints(16), ints(16),
+            words(8, 6), words(8, 6), words(8, 6), words(8, 6), words(8, 3), words(8, 3),
+            words(), words(8), words(), words(8),
+            pltpu.SemaphoreType.DMA((5, 8)),
+            pltpu.SemaphoreType.DMA((5, 8)),
+        ],
+        compiler_params=pltpu.CompilerParams(collective_id=0, has_side_effects=True),
+    )(cell, vehicle, speed)
+
+
+def per_device(cell, vehicle, speed):
+    shaped = [x.reshape(32, 8, 128) for x in (cell, vehicle, speed)]
+    best, ident, flags = sparse_path(*shaped)
+    return lax.cond(
+        flags[0, 0] > 0.0,
+        lambda: dense_path(cell, vehicle, speed),
+        lambda: (best.reshape(1024), ident.reshape(1024)),
+    )
 
 
 def solution(mesh):

time: 697 us -> 52.9 us (0.08)
  other arithmetic: 373 us -> 0 us
  local copies, waits for them, and re-layouts: 181 us -> 2.37 us
  waiting for transfers between devices: 86.9 us -> 0 us
  starting transfers between devices: 52.3 us -> 0 us
  Pallas kernels: 0 us -> 48.8 us
    another operation x11 -> x0, other arithmetic: 360 us -> none  [the longest x1 176 us: per_device(): local_ident = jnp.full((CELLS,), VEHICLES, jnp.int32).at[cell].min(chosen)]
    gather x1 -> x0, local copies, waits for them, and re-layouts: 181 us -> none  [per_device(): chosen = jnp.where(speed == local_best[cell], vehicle, VEHICLES)]
    ppermute x9 -> x0, waiting for transfers between devices: 86.9 us -> none  [swapped(): return lax.ppermute(block, axis, route)]
    ppermute x9 -> x0, starting transfers between devices: 52.3 us -> none  [swapped(): return lax.ppermute(block, axis, route)]
    pallas_call x0 -> x1, Pallas kernels: none -> 48.8 us  [sparse_path(): pl.pallas_call(exchange_kernel, out_shape=(jax.ShapeDtypeStruct((8, 128),...]
    select_n x10 -> x0, other arithmetic: 8.15 us -> none  [the longest x8 7.53 us: combine(): jnp.where(speed_a > speed_b, first[1], jnp.where(speed_b > speed_a, secon...]
  transfers between devices with their start and end apart: 9 -> 0, of which waited for: 9 -> 0; matrix products, arithmetic and copies ran while one was open for 0% -> 0% of each run, Pallas kernels for 0% -> 0%
where the time goes in v1:
time: 52.9 us; the launch traced here: 52.7 us
  Pallas kernels  48.8 us (92%)
  local copies, waits for them, and re-layouts  2.37 us (4%)
  between operations  1.3 us (2%)
    pallas_call x1, Pallas kernels, sparse_path(): pl.pallas_call(exchange_kernel, out_shape=(jax.ShapeDtypeStruct((8, 128),...  48.8 us
    unnamed x2, local copies, waits for them, and re-layouts  1.19 us
    slice x1, local copies, waits for them, and re-layouts, per_device(): flags[0, 0] > 0.0  1.19 us

profile of v1, /device:TPU:1, one launch (start us, length us, event | category | flops | bytes accessed | tf_op | source)
XLA Modules:
  0.0 52.7 jit_solution(2128781570890018775)
XLA Ops:
  0.6 48.8 %shard_map.54 = (f32[8,128]{1,0:T(8,128)S(1)}, s32[8,128]{1,0:T(8,128)S(1)}, f32[8,128]{1,0:T(8,128)}) custom-call(s32[32,8,128]{2,1,0:T(8,128)} %bitcast.13, s32[32,8,128]{2,1,0:T(8,128)} %bitcast.14, f32[32,8,128]{2,1,0:T(8,128)} %bitcast.15), custom_call_target="tpu_custom_call" | custom-call | tf_op jit(solution)/shard_map/pallas_call | solution.py:551
  49.5 1.2 %slice.129 = f32[1,1]{1,0:T(1,128)} slice(f32[8,128]{1,0:T(8,128)} %get-tuple-element.20), slice={[0:1], [0:1]} | slice | bytes 8 | tf_op jit(solution)/shard_map/slice | solution.py:575
  51.3 0.2 conditional.1
  51.5 0.6 %copy.15 = f32[1024]{0:T(1024)} copy(f32[1024]{0:T(1024)S(1)} %get-tuple-element.72) | data formatting | bytes 8192
  52.1 0.6 %copy.16 = s32[1024]{0:T(1024)} copy(s32[1024]{0:T(1024)S(1)} %get-tuple-element.73) | data formatting | bytes 8192
